TPU v7x, 32 devices: a 4x4x1 block of a 4x4x8 slice. The times are simulated.
32 devices in a mesh: dp: 1 (over z), cfg: 4 (over y), tp: 8 (over x, core).
Axes of the slice: x: 4, y: 4, z: 1, core: 2. Of those that a mesh axis runs over, the one named last changes fastest.
The devices are a block of a 4x4x8 slice.
Arguments:
- hidden: bfloat16 [4, 4096, 1152], P(('dp', 'cfg'))
- caption: bfloat16 [4, 300, 1152], P(('dp', 'cfg'))
- cap_len: int32 [4], P(('dp', 'cfg'))
- t_block: bfloat16 [2, 6912], P('dp')
- t_embed: bfloat16 [2, 1152], P('dp')
- x_t: float32 [2, 128, 128, 4], P('dp')
- alpha_bar: float32 [2, 2], P('dp')
- mod_table: bfloat16 [2, 6, 1152], replicated
- w_qkv: bfloat16 [2, 1152, 3, 16, 72], P(None, None, None, 'tp')
- w_proj: bfloat16 [2, 16, 72, 1152], P(None, 'tp')
- w_cq: bfloat16 [2, 1152, 16, 72], P(None, None, 'tp')
- w_ckv: bfloat16 [2, 1152, 2, 16, 72], P(None, None, None, 'tp')
- w_cproj: bfloat16 [2, 16, 72, 1152], P(None, 'tp')
- w_fc1: bfloat16 [2, 1152, 4608], P(None, None, 'tp')
- w_fc2: bfloat16 [2, 4608, 1152], P(None, 'tp')
- final_table: bfloat16 [2, 1152], replicated
- w_out: bfloat16 [1152, 32], replicated
- b_out: bfloat16 [32], replicated
Outputs:
- output: float32 [2, 128, 128, 4], P('dp')
All inputs are finite; a program needn't handle non-finite values.
Results may differ from a plain program's by a relative error of at most 0.013431.
Values are sent between devices in bfloat16 or wider.
A program may use at most 768 MiB of HBM per device.

v0:
```python
import jax
import jax.numpy as jnp
from jax import lax
from jax.sharding import PartitionSpec as P

GUIDANCE = 4.5
LN_EPS = 1e-6


def layer_norm(values):
    mean_val = jnp.mean(values, axis=-1, keepdims=True)
    centered = values - mean_val
    variance = jnp.mean(centered * centered, axis=-1, keepdims=True)
    return centered * lax.rsqrt(variance + LN_EPS)


def attention(queries, key_vecs, values, key_mask):
    qk_scale = queries.shape[-1] ** -0.5
    scores = jnp.einsum('rqhd,rkhd->rhqk', queries, key_vecs, preferred_element_type=jnp.float32) * qk_scale
    if key_mask is not None:
        scores = jnp.where(key_mask, scores, -1e30)
    attn_prob = jax.nn.softmax(scores, axis=-1).astype(jnp.bfloat16)
    return jnp.einsum('rhqk,rkhd->rqhd', attn_prob, values, preferred_element_type=jnp.float32).astype(jnp.bfloat16)


def tp_block(residual, caption, key_mask, mod_rows, w_qkv, w_proj, w_cq, w_ckv, w_cproj, w_fc1, w_fc2):
    attn_in = (layer_norm(residual) * (1.0 + mod_rows[:, None, 1]) + mod_rows[:, None, 0]).astype(jnp.bfloat16)
    qkv_out = jnp.einsum('rnd,dshe->rnshe', attn_in, w_qkv, preferred_element_type=jnp.float32).astype(jnp.bfloat16)
    self_o = attention(qkv_out[:, :, 0], qkv_out[:, :, 1], qkv_out[:, :, 2], None)
    self_part = jnp.einsum('rnhe,hed->rnd', self_o, w_proj, preferred_element_type=jnp.float32).astype(jnp.bfloat16)
    residual = residual + mod_rows[:, None, 2] * lax.psum(self_part, 'tp').astype(jnp.float32)
    cross_q = jnp.einsum('rnd,dhe->rnhe', residual.astype(jnp.bfloat16), w_cq, preferred_element_type=jnp.float32).astype(jnp.bfloat16)
    cross_kv = jnp.einsum('rtd,dshe->rtshe', caption, w_ckv, preferred_element_type=jnp.float32).astype(jnp.bfloat16)
    cross_o = attention(cross_q, cross_kv[:, :, 0], cross_kv[:, :, 1], key_mask)
    cross_part = jnp.einsum('rnhe,hed->rnd', cross_o, w_cproj, preferred_element_type=jnp.float32).astype(jnp.bfloat16)
    residual = residual + lax.psum(cross_part, 'tp').astype(jnp.float32)
    mlp_in = (layer_norm(residual) * (1.0 + mod_rows[:, None, 4]) + mod_rows[:, None, 3]).astype(jnp.bfloat16)
    mlp_hidden = jax.nn.gelu(jnp.einsum('rnd,df->rnf', mlp_in, w_fc1, preferred_element_type=jnp.float32), approximate=True).astype(jnp.bfloat16)
    mlp_part = jnp.einsum('rnf,fd->rnd', mlp_hidden, w_fc2, preferred_element_type=jnp.float32).astype(jnp.bfloat16)
    return residual + mod_rows[:, None, 5] * lax.psum(mlp_part, 'tp').astype(jnp.float32)


def final_layer(residual, final_table, emb_rows, w_out, b_out, side_len):
    shift_scale = final_table.astype(jnp.float32)[None] + emb_rows[:, None]
    final_in = (layer_norm(residual) * (1.0 + shift_scale[:, None, 1]) + shift_scale[:, None, 0]).astype(jnp.bfloat16)
    out_tok = jnp.einsum('rnd,dc->rnc', final_in, w_out, preferred_element_type=jnp.float32) + b_out.astype(jnp.float32)
    n_rows = residual.shape[0]
    grid_side = side_len // 2
    patches = out_tok.reshape(n_rows, grid_side, grid_side, 2, 2, 8)[:, :, :, :, :, :4]
    return patches.transpose(0, 1, 3, 2, 4, 5).reshape(n_rows, side_len, side_len, 4)


def guidance_mix(eps_all):
    n_images = eps_all.shape[0] // 2
    eps_uncond = eps_all[n_images:]
    return eps_uncond + GUIDANCE * (eps_all[:n_images] - eps_uncond)


def ddim_update(guided, x_t, alpha_bar):
    abar_t = alpha_bar[:, 0][:, None, None, None]
    abar_prev = alpha_bar[:, 1][:, None, None, None]
    x_zero = (x_t - jnp.sqrt(1.0 - abar_t) * guided) / jnp.sqrt(abar_t)
    return jnp.sqrt(abar_prev) * x_zero + jnp.sqrt(1.0 - abar_prev) * guided


def solution(mesh):
    row_spec = P(('dp', 'cfg'))
    part_spec = P('dp')
    in_specs = (row_spec, row_spec, row_spec, part_spec, part_spec, part_spec, part_spec, P(),
                P(None, None, None, 'tp'), P(None, 'tp'), P(None, None, 'tp'), P(None, None, None, 'tp'),
                P(None, 'tp'), P(None, None, 'tp'), P(None, 'tp'), P(), P(), P())

    def local_step(hidden, caption, cap_len, t_block, t_embed, x_t, alpha_bar, mod_table, w_qkv, w_proj, w_cq, w_ckv, w_cproj, w_fc1, w_fc2, final_table, w_out, b_out):
        n_rows = hidden.shape[0]
        model_dim = hidden.shape[2]
        row_start = (lax.axis_index('cfg') * n_rows) % t_block.shape[0]
        t_rows = lax.dynamic_slice_in_dim(t_block, row_start, n_rows, axis=0).astype(jnp.float32).reshape(n_rows, 6, model_dim)
        emb_rows = lax.dynamic_slice_in_dim(t_embed, row_start, n_rows, axis=0).astype(jnp.float32)
        key_mask = (jnp.arange(caption.shape[1])[None, :] < cap_len[:, None])[:, None, None, :]
        residual = hidden.astype(jnp.float32)
        for layer_idx in range(mod_table.shape[0]):
            mod_rows = mod_table[layer_idx].astype(jnp.float32)[None] + t_rows
            residual = tp_block(residual, caption, key_mask, mod_rows, w_qkv[layer_idx], w_proj[layer_idx], w_cq[layer_idx], w_ckv[layer_idx], w_cproj[layer_idx], w_fc1[layer_idx], w_fc2[layer_idx])
        eps_local = final_layer(residual, final_table, emb_rows, w_out, b_out, x_t.shape[1])
        eps_all = lax.all_gather(eps_local, 'cfg', axis=0, tiled=True)
        return ddim_update(guidance_mix(eps_all), x_t, alpha_bar)

    return jax.shard_map(local_step, mesh=mesh, in_specs=in_specs, out_specs=part_spec, check_vma=False)
```

profile of v0, /device:TPU:98, one launch (start us, length us, event | category | flops | bytes accessed | tf_op | source)
XLA Modules:
  0.0 1171.4 jit_solution(1725435905202995143)
XLA Ops:
  17.7 8.3 fusion.65
  28.3 56.5 %fusion.200 = (f32[2,4096]{1,0:T(2,128)S(1)}, f32[2,4096,4096]{1,2,0:T(8,128)}) fusion(bf16[1,4096,3,2,72]{1,4,3,2,0:T(8,128)(2,1)} %convert_bitcast_fusion.1), kind=kOutput, calls=%fused_computation.245 | convolution fusion | flops 4932505600 | bytes 136609792 | tf_op jit(solution)/shard_map/sub | solution.py:22
  84.7 43.6 %fusion.122 = bf16[4096,2,72]{0,2,1:T(8,128)(2,1)} fusion(f32[2,4096,4096]{1,2,0:T(8,128)} %get-tuple-element.38, f32[2,4096]{1,0:T(2,128)S(1)} %get-tuple-element.37, bf16[1,4096,3,2,72]{1,4,3,2,0:T(8,128)(2,1)} %convert_bitcast_fusion.1), kind=kOutput, calls=%fused_computation.135 | convolution fusion | flops 4899536896 | bytes 136609792 | tf_op jit(solution)/shard_map/rhqk,rkhd->rqhd/dot_general | solution.py:23
  128.3 8.0 fusion.27
  139.5 106.5 %all-reduce.7.cloned.1.call-done = bf16[1,4096,1152]{2,1,0:T(8,128)(2,1)} async-done(((bf16[1,4096,1152]{2,1,0:T(8,128)(2,1)}), bf16[1,4096,1152]{2,1,0:T(8,128)(2,1)}) %all-reduce.7.cloned.1.call-update) | async-done | bytes 9437200 | tf_op jit(solution)/shard_map/psum | solution.py:31
  246.0 11.4 fusion.52
  257.4 9.3 fusion.201
  266.7 9.1 fusion.28
  276.4 108.2 %all-reduce.9.cloned.1.call-done = bf16[1,4096,1152]{2,1,0:T(8,128)(2,1)} async-done(((bf16[1,4096,1152]{2,1,0:T(8,128)(2,1)}), bf16[1,4096,1152]{2,1,0:T(8,128)(2,1)}) %all-reduce.9.cloned.1.call-update) | async-done | bytes 9437200 | tf_op jit(solution)/shard_map/psum | solution.py:36
  384.6 11.0 fusion.193
  396.4 9.4 multiply_reduce_fusion.5
  405.8 23.8 %fusion.25 = bf16[1,4096,1152]{2,1,0:T(8,128)(2,1)} fusion(f32[1152]{0:T(1024)S(1)} %copy-done.23, f32[1152]{0:T(1024)S(1)} %copy-done.22, f32[4096]{0:T(1024)S(1)} %add_rsqrt_fusion.3, f32[4096]{0:T(1024)S(1)} %broadcast_multiply_fusion.3, bf16[2,576,1152]{2,1,0:T(8,128)(2,1)} %param.32, bf16[2,1152,576]{1,2,0:T(8,128)(2,1)} %param.31, ...), kind=kOutput, calls=%fused_computation.49 | convolution fusion | flops 10949492736 | bytes 40449536 | tf_op jit(solution)/shard_map/rnf,fd->rnd/dot_general | solution.py:39
  429.9 108.5 %all-reduce.11.cloned.1.call-done = bf16[1,4096,1152]{2,1,0:T(8,128)(2,1)} async-done(((bf16[1,4096,1152]{2,1,0:T(8,128)(2,1)}), bf16[1,4096,1152]{2,1,0:T(8,128)(2,1)}) %all-reduce.11.cloned.1.call-update) | async-done | bytes 9437200 | tf_op jit(solution)/shard_map/psum | solution.py:40
  538.4 20.2 %fusion.195 = (f32[4096]{0:T(1024)S(1)}, f32[1,4096,1152]{2,1,0:T(8,128)}) fusion(bf16[1,4096,1152]{2,1,0:T(8,128)(2,1)} %all-reduce.11.cloned.1.call-done, f32[1152]{0:T(1024)S(1)} %copy-done.16, bf16[1,4096,1152]{2,1,0:T(8,128)(2,1)} %all-reduce.9.cloned.1.call-done, bf16[1,4096,1152]{2,1,0:T(8,128)(2,1)} %all-reduce.7.cloned.1.call-done, ...), kind=kLoop, calls=%fused_computation.240 | loop fusion | flops 47181824 | bytes 56648704 | tf_op jit(solution)/shard_map/reduce_sum | solution.py:11
  558.6 8.5 multiply_reduce_fusion.4
  567.1 10.2 fusion.58
  579.7 56.5 %fusion.204 = (f32[2,4096]{1,0:T(2,128)S(1)}, f32[2,4096,4096]{1,2,0:T(8,128)}) fusion(bf16[1,4096,3,2,72]{1,4,3,2,0:T(8,128)(2,1)} %convert_bitcast_fusion), kind=kOutput, calls=%fused_computation.247 | convolution fusion | flops 4932505600 | bytes 136609792 | tf_op jit(solution)/shard_map/sub | solution.py:22
  636.2 43.5 %fusion.123 = bf16[4096,2,72]{0,2,1:T(8,128)(2,1)} fusion(f32[2,4096,4096]{1,2,0:T(8,128)} %get-tuple-element.42, f32[2,4096]{1,0:T(2,128)S(1)} %get-tuple-element.41, bf16[1,4096,3,2,72]{1,4,3,2,0:T(8,128)(2,1)} %convert_bitcast_fusion), kind=kOutput, calls=%fused_computation.136 | convolution fusion | flops 4899536896 | bytes 136609792 | tf_op jit(solution)/shard_map/rhqk,rkhd->rqhd/dot_general | solution.py:23
  679.7 8.0 fusion.29
  689.0 107.4 %all-reduce.13.cloned.1.call-done = bf16[1,4096,1152]{2,1,0:T(8,128)(2,1)} async-done(((bf16[1,4096,1152]{2,1,0:T(8,128)(2,1)}), bf16[1,4096,1152]{2,1,0:T(8,128)(2,1)}) %all-reduce.13.cloned.1.call-update) | async-done | bytes 9437200 | tf_op jit(solution)/shard_map/psum | solution.py:31
  796.5 10.8 fusion.33
  807.3 8.5 fusion.205
  815.8 9.1 fusion.30
  825.1 108.7 %all-reduce.15.cloned.1.call-done = bf16[1,4096,1152]{2,1,0:T(8,128)(2,1)} async-done(((bf16[1,4096,1152]{2,1,0:T(8,128)(2,1)}), bf16[1,4096,1152]{2,1,0:T(8,128)(2,1)}) %all-reduce.15.cloned.1.call-update) | async-done | bytes 9437200 | tf_op jit(solution)/shard_map/psum | solution.py:36
  933.8 20.1 %fusion.194 = (f32[4096]{0:T(1024)S(1)}, f32[1,4096,1152]{2,1,0:T(8,128)}) fusion(bf16[1,4096,1152]{2,1,0:T(8,128)(2,1)} %all-reduce.15.cloned.1.call-done, f32[1,4096,1152]{2,1,0:T(8,128)} %get-tuple-element.26, bf16[1,4096,1152]{2,1,0:T(8,128)(2,1)} %all-reduce.13.cloned.1.call-done, f32[1152]{0:T(1024)S(1)} %copy-done.12), kind=kLoop, calls=%fused_computation.239 | loop fusion | flops 28307456 | bytes 56644096 | tf_op jit(solution)/shard_map/reduce_sum | solution.py:11
  953.9 8.4 multiply_reduce_fusion.3
  962.4 20.8 %fusion.26 = bf16[1,4096,1152]{2,1,0:T(8,128)(2,1)} fusion(f32[1,4096,1152]{2,1,0:T(8,128)} %get-tuple-element.24, f32[1152]{0:T(1024)S(1)} %copy-done.18, f32[1152]{0:T(1024)S(1)} %copy-done.19, f32[4096]{0:T(1024)S(1)} %add_rsqrt_fusion.1, f32[4096]{0:T(1024)S(1)} %broadcast_multiply_fusion.1, bf16[2,576,1152]{2,1,0:T(8,128)(2,1)} %param.32, ...), kind=kOutput, calls=%fused_computation.50 | convolution fusion | flops 10921181184 | bytes 31007744 | tf_op jit(solution)/shard_map/rnf,fd->rnd/dot_general | solution.py:39
  983.4 108.6 %all-reduce.17.cloned.1.call-done = bf16[1,4096,1152]{2,1,0:T(8,128)(2,1)} async-done(((bf16[1,4096,1152]{2,1,0:T(8,128)(2,1)}), bf16[1,4096,1152]{2,1,0:T(8,128)(2,1)}) %all-reduce.17.cloned.1.call-update) | async-done | bytes 9437200 | tf_op jit(solution)/shard_map/psum | solution.py:40
  1092.0 12.5 %fusion.97 = f32[4096]{0:T(1024)S(1)} fusion(f32[1,4096,1152]{2,1,0:T(8,128)} %get-tuple-element.24, bf16[1,4096,1152]{2,1,0:T(8,128)(2,1)} %all-reduce.17.cloned.1.call-done, f32[1152]{0:T(1024)S(1)} %copy-done.15), kind=kLoop, calls=%fused_computation.120 | loop fusion | flops 18870272 | bytes 28332544 | tf_op jit(solution)/shard_map/reduce_sum | solution.py:11
  1104.6 10.2 multiply_reduce_fusion.2
  1123.3 8.8 copy.47
  1138.3 23.6 %all-gather.2.cloned.1.call-done = f32[4,128,128,4]{2,1,3,0:T(8,128)} async-done(((f32[1,128,128,4]{2,1,3,0:T(8,128)}), f32[4,128,128,4]{2,1,3,0:T(8,128)}) %all-gather.2.cloned.1.call-update) | async-done | bytes 1048592 | tf_op jit(solution)/shard_map/all_gather | solution.py:85
  (131 shorter events, 38.7 us)
Async XLA Ops:
  6.5 131.6 %copy-start = (bf16[1,300,1152]{2,1,0:T(8,128)(2,1)S(1)}, bf16[1,300,1152]{2,1,0:T(8,128)(2,1)}, u32[]{:S(2)}) copy-start(bf16[1,300,1152]{2,1,0:T(8,128)(2,1)} %param.19) | copy-start | bytes 2073604
  6.6 239.4 %all-reduce.7.cloned.1.call-start = ((), (), s32[]{:S(2)}) async-start(), calls=%async_computation | async-start | bytes 18874368 | tf_op jit(solution)/shard_map/psum | solution.py:31
  84.7 43.6 %copy-start.27 = (bf16[2,2,72,1152]{3,2,1,0:T(8,128)(2,1)S(1)}, bf16[2,2,72,1152]{3,2,1,0:T(8,128)(2,1)}, u32[]{:S(2)}) copy-start(bf16[2,2,72,1152]{3,2,1,0:T(8,128)(2,1)} %param.27) | copy-start | bytes 1990660
  136.3 109.7 %copy-start.13 = (f32[1152]{0:T(1024)S(1)}, f32[1152]{0:T(1024)}, u32[]{:S(2)}) copy-start(f32[1152]{0:T(1024)} %get-tuple-element.45) | copy-start | bytes 13828
  136.4 248.2 %all-reduce.9.cloned.1.call-start = ((), (), s32[]{:S(2)}) async-start(), calls=%async_computation.1 | async-start | bytes 18874368 | tf_op jit(solution)/shard_map/psum | solution.py:36
  137.2 120.2 %copy-start.32 = (pred[300]{0:T(512)(128)(4,1)}, pred[300]{0:T(512)(128)(4,1)S(1)}, u32[]{:S(2)}) copy-start(pred[300]{0:T(512)(128)(4,1)S(1)} %iota_compare_fusion) | copy-start | bytes 904
  275.8 262.6 %all-reduce.11.cloned.1.call-start = ((), (), s32[]{:S(2)}) async-start(), calls=%async_computation.2 | async-start | bytes 18874368 | tf_op jit(solution)/shard_map/psum | solution.py:40
  384.6 11.8 %copy-start.2 = (bf16[1,4096,1152]{2,1,0:T(8,128)(2,1)S(1)}, bf16[1,4096,1152]{2,1,0:T(8,128)(2,1)}, u32[]{:S(2)}) copy-start(bf16[1,4096,1152]{2,1,0:T(8,128)(2,1)} %all-reduce.9.cloned.1.call-done) | copy-start | bytes 28311556
  396.4 9.4 copy-start.22
  396.4 9.4 copy-start.23
  405.8 132.6 %copy-start.16 = (f32[1152]{0:T(1024)S(1)}, f32[1152]{0:T(1024)}, u32[]{:S(2)}) copy-start(f32[1152]{0:T(1024)} %get-tuple-element.50) | copy-start | bytes 13828
  429.6 366.9 %all-reduce.13.cloned.1.call-start = ((), (), s32[]{:S(2)}) async-start(), calls=%async_computation.3 | async-start | bytes 18874368 | tf_op jit(solution)/shard_map/psum | solution.py:31
  636.1 43.5 %copy-start.28 = (bf16[2,2,72,1152]{3,2,1,0:T(8,128)(2,1)S(1)}, bf16[2,2,72,1152]{3,2,1,0:T(8,128)(2,1)}, u32[]{:S(2)}) copy-start(bf16[2,2,72,1152]{3,2,1,0:T(8,128)(2,1)} %param.27) | copy-start | bytes 1990660
  679.7 116.8 %copy-start.6 = (bf16[1,1152,2,72]{1,3,2,0:T(8,128)(2,1)S(1)}, bf16[1,1152,2,72]{1,3,2,0:T(8,128)(2,1)}, u32[]{:S(2)}) copy-start(bf16[1,1152,2,72]{1,3,2,0:T(8,128)(2,1)} %get-tuple-element.32) | copy-start | bytes 995332
  679.7 116.8 %copy-start.12 = (f32[1152]{0:T(1024)S(1)}, f32[1152]{0:T(1024)}, u32[]{:S(2)}) copy-start(f32[1152]{0:T(1024)} %get-tuple-element.10) | copy-start | bytes 13828
  687.7 246.1 %all-reduce.15.cloned.1.call-start = ((), (), s32[]{:S(2)}) async-start(), calls=%async_computation.4 | async-start | bytes 18874368 | tf_op jit(solution)/shard_map/psum | solution.py:36
  796.5 10.9 copy-start.33
  825.0 267.0 %all-reduce.17.cloned.1.call-start = ((), (), s32[]{:S(2)}) async-start(), calls=%async_computation.5 | async-start | bytes 18874368 | tf_op jit(solution)/shard_map/psum | solution.py:40
  962.4 20.9 %copy-start.31 = (bf16[32]{0:T(256)(128)(2,1)S(1)}, bf16[32]{0:T(256)(128)(2,1)}, u32[]{:S(2)}) copy-start(bf16[32]{0:T(256)(128)(2,1)} %param.35) | copy-start | bytes 196
  962.4 21.0 %copy-start.24 = (bf16[2,1152]{1,0:T(2,128)(2,1)S(1)}, bf16[2,1152]{1,0:T(2,128)(2,1)}, u32[]{:S(2)}) copy-start(bf16[2,1152]{1,0:T(2,128)(2,1)} %param.22) | copy-start | bytes 13828
  962.4 21.0 %copy-start.25 = (bf16[2,1152]{1,0:T(2,128)(2,1)S(1)}, bf16[2,1152]{1,0:T(2,128)(2,1)}, u32[]{:S(2)}) copy-start(bf16[2,1152]{1,0:T(2,128)(2,1)} %param.33) | copy-start | bytes 13828
  962.4 129.6 %copy-start.15 = (f32[1152]{0:T(1024)S(1)}, f32[1152]{0:T(1024)}, u32[]{:S(2)}) copy-start(f32[1152]{0:T(1024)} %get-tuple-element.5) | copy-start | bytes 13828
  983.2 178.6 %all-gather.2.cloned.1.call-start = ((), (), s32[]{:S(2)}) async-start(), calls=%async_computation.6 | async-start | bytes 1310720 | tf_op jit(solution)/shard_map/all_gather | solution.py:85
  1092.0 12.6 %copy-start.3 = (bf16[1,4096,1152]{2,1,0:T(8,128)(2,1)S(1)}, bf16[1,4096,1152]{2,1,0:T(8,128)(2,1)}, u32[]{:S(2)}) copy-start(bf16[1,4096,1152]{2,1,0:T(8,128)(2,1)} %all-reduce.17.cloned.1.call-done) | copy-start | bytes 28311556
  1092.0 22.8 %slice-start = ((s8[18874368]{0:T(1024)(128)(4,1)}), s8[4194304]{0:T(1024)(128)(4,1)S(1)}, s32[]{:S(2)}) async-start(s8[18874368]{0:T(1024)(128)(4,1)} %bitcast.247), calls=%async_computation.7 | async-start | bytes 8388608
  1092.0 22.8 %slice-start.1 = ((s8[18874368]{0:T(1024)(128)(4,1)}), s8[4194304]{0:T(1024)(128)(4,1)S(1)}, s32[]{:S(2)}) async-start(s8[18874368]{0:T(1024)(128)(4,1)} %bitcast.247), calls=%async_computation.8 | async-start | bytes 8388608
  1092.0 22.9 %slice-start.2 = ((s8[18874368]{0:T(1024)(128)(4,1)}), s8[4194304]{0:T(1024)(128)(4,1)S(1)}, s32[]{:S(2)}) async-start(s8[18874368]{0:T(1024)(128)(4,1)} %bitcast.247), calls=%async_computation.9 | async-start | bytes 8388608
  1104.6 10.3 slice-start.3
  1104.6 10.4 slice-start.4
  1104.6 10.3 copy-start.30
  1122.8 15.2 %copy-start.26 = (f32[2,2]{1,0:T(2,128)S(1)}, f32[2,2]{1,0:T(2,128)}, u32[]{:S(2)}) copy-start(f32[2,2]{1,0:T(2,128)} %param.24) | copy-start | bytes 52
  1122.8 39.0 %copy-start.10 = (f32[2,128,128,4]{2,3,1,0:T(4,128)S(1)}, f32[2,128,128,4]{2,3,1,0:T(4,128)}, u32[]{:S(2)}) copy-start(f32[2,128,128,4]{2,3,1,0:T(4,128)} %param.23) | copy-start | bytes 1572868
  (14 other events, 113.7 us)
Sparse Core Ops, SparseCore 0:
  136.5 109.4 all-reduce.6
  275.9 108.5 all-reduce.8
  429.7 108.5 all-reduce.10
  687.8 108.6 all-reduce.12
  825.2 108.6 all-reduce.14
  983.4 108.6 all-reduce.16
  1138.1 23.6 all-gather.1
where the time goes:
time: 1180 us; the launch traced here: 1170 us
  waiting for transfers between devices  672 us (57%)
  matrix products  346 us (29%)
  other arithmetic  116 us (10%)
  local copies, waits for them, and re-layouts  21.5 us (2%)
  between operations  15 us (1%)
    psum x2, waiting for transfers between devices, tp_block(): lax.psum(mlp_part, 'tp').astype(jnp.float32)  217 us
    psum x2, waiting for transfers between devices, tp_block(): residual = residual + lax.psum(cross_part, 'tp').astype(jnp.float32)  217 us
    psum x2, waiting for transfers between devices, tp_block(): lax.psum(self_part, 'tp').astype(jnp.float32)  214 us
    sub x4, matrix products, attention(): attn_prob = jax.nn.softmax(scores, axis=-1).astype(jnp.bfloat16)  131 us
    dot_general x2, matrix products, attention(): jnp.einsum('rhqk,rkhd->rqhd', attn_prob, values, preferred_element_type=j...  87.1 us
    reduce_sum x5, other arithmetic, layer_norm(): mean_val = jnp.mean(values, axis=-1, keepdims=True)  69 us
    dot_general x2, matrix products, tp_block(): jnp.einsum('rnf,fd->rnd', mlp_hidden, w_fc2, preferred_element_type=jnp.f...  44.5 us
    unnamed x6, matrix products  41.8 us
  transfers between devices with their start and end apart: 7, of which 7 were waited for; matrix products, arithmetic and copies ran while one was open for 0% of the time, Pallas kernels for 0%

commit v1 on v0

v1 whole, which is shorter than its diff:
```python
import functools

import jax
import jax.numpy as jnp
from jax import lax
from jax.experimental import pallas as pl
from jax.experimental.pallas import tpu as pltpu
from jax.sharding import PartitionSpec as P

GUIDANCE = 4.5
LN_EPS = 1e-6
LOG2E = 1.4426950408889634
NT = (((1,), (1,)), ((), ()))
BF = jnp.bfloat16
F32 = jnp.float32


def layer_norm(values):
    mean_val = jnp.mean(values, axis=-1, keepdims=True)
    centered = values - mean_val
    variance = jnp.mean(centered * centered, axis=-1, keepdims=True)
    return centered * lax.rsqrt(variance + LN_EPS)


def dot(a, b):
    return jnp.dot(a, b, preferred_element_type=F32)


def dot_nt(a, b):
    return lax.dot_general(a, b, NT, preferred_element_type=F32)


def attn_kernel(cfg, src_ref, mod_ref, w_ref, o_ref, x_vm, q_vm, k_vm, vt_vm, s0, s1, sems):
    n_tok, n_dest, heads, hd, tok_blk, qb, kb, use_ln = cfg
    n_blk = n_tok // tok_blk
    hw = heads * hd
    scale = hd ** -0.5 * LOG2E

    def load(i):
        rows = pl.ds(pl.multiple_of(i * tok_blk, tok_blk), tok_blk)
        return pltpu.make_async_copy(src_ref.at[rows], x_vm.at[rows], sems.at[i])

    for i in range(n_blk):
        load(i).start()
    row_id = lax.broadcasted_iota(jnp.int32, (80 - hd, n_tok), 0)
    for h in range(heads):
        vt_vm[h, hd:, :] = jnp.where(row_id == 0, 1.0, 0.0).astype(BF)

    def qkv_step(i, carry):
        load(i).wait()
        rows = pl.ds(pl.multiple_of(i * tok_blk, tok_blk), tok_blk)
        x = x_vm[rows, :]
        if use_ln:
            x = (layer_norm(x.astype(F32)) * (1.0 + mod_ref[1:2, :]) + mod_ref[0:1, :]).astype(BF)
        qkv = dot(x, w_ref[...])
        q = qkv[:, :hw] * scale
        lane = lax.broadcasted_iota(jnp.int32, q.shape, 1)
        for h in range(heads):
            q_vm[h, rows, :] = jnp.where((lane >= h * hd) & (lane < (h + 1) * hd), q, 0.0).astype(BF)
        k_vm[rows, :] = qkv[:, hw:2 * hw].astype(BF)
        vt = qkv[:, 2 * hw:].T
        for h in range(heads):
            vt_vm[h, :hd, rows] = vt[h * hd:(h + 1) * hd, :].astype(BF)
        return carry

    lax.fori_loop(0, n_blk, qkv_step, 0)

    bufs = (s0, s1)
    n_kb = n_tok // kb
    dest_tok = n_tok // n_dest

    def q_step(i, carry):
        h = lax.rem(i, heads)
        qi = lax.div(i, heads)
        q = q_vm[h, pl.ds(pl.multiple_of(qi * qb, qb), qb), :]

        def scores(j, dst):
            s = dot_nt(k_vm[j * kb:(j + 1) * kb, :], q)
            dst[...] = s
            return jnp.max(jnp.max(s.reshape(kb // 8, 8, qb), axis=0), axis=0, keepdims=True)

        m = scores(0, bufs[0])
        acc = None
        for j in range(n_kb):
            blk_max = scores(j + 1, bufs[(j + 1) % 2]) if j + 1 < n_kb else None
            p = jnp.exp2(bufs[j % 2][...] - m).astype(BF)
            pv = dot(vt_vm[h, :, j * kb:(j + 1) * kb], p)
            acc = pv if acc is None else acc + pv
            if blk_max is not None:
                m_new = jnp.maximum(m, blk_max)
                acc = acc * jnp.exp2(m - m_new)
                m = m_new
        o = (acc[:hd] / acc[hd:hd + 1]).astype(BF)
        for u in range(qb // dest_tok):
            o_ref[qi * (qb // dest_tok) + u, h, :, :] = o[:, u * dest_tok:(u + 1) * dest_tok]
        return carry

    lax.fori_loop(0, heads * (n_tok // qb), q_step, 0)


def self_attention(src, mods, w, n_dest, heads, hd, use_ln):
    n_tok, dim = src.shape
    tok_blk, qb, kb = 512, 1024, 512
    cfg = (n_tok, n_dest, heads, hd, tok_blk, qb, kb, use_ln)
    vmem = pl.BlockSpec(memory_space=pltpu.VMEM)
    return pl.pallas_call(
        functools.partial(attn_kernel, cfg),
        out_shape=jax.ShapeDtypeStruct((n_dest, heads, hd, n_tok // n_dest), BF),
        in_specs=[pl.BlockSpec(memory_space=pl.ANY), vmem, vmem],
        out_specs=vmem,
        scratch_shapes=[
            pltpu.VMEM((n_tok, dim), BF),
            pltpu.VMEM((heads, n_tok, heads * hd), BF),
            pltpu.VMEM((n_tok, heads * hd), BF),
            pltpu.VMEM((heads, 80, n_tok), BF),
            pltpu.VMEM((kb, qb), F32),
            pltpu.VMEM((kb, qb), F32),
            pltpu.SemaphoreType.DMA((n_tok // tok_blk,)),
        ],
        compiler_params=pltpu.CompilerParams(vmem_limit_bytes=60 << 20),
        cost_estimate=pl.CostEstimate(flops=30 * 10 ** 9, bytes_accessed=20 * 10 ** 6, transcendentals=0),
    )(src, mods, w)


def tok_kernel(cfg, o_ref, x_ref, g_ref, kc_ref, vc_ref, mod_ref, wo_ref, bo_ref, *refs):
    tp, hd, rows_p, rows_f, last = cfg
    if last:
        (e_ref, wp, wcp, wcq, w1, w2, x_vm, h_vm, q_vm, sems, xsem) = refs
    else:
        (xo_ref, a_ref, wp, wcp, wcq, w1, w2, x_vm, h_vm, q_vm, sems, xsem) = refs
    n_tok, dim = x_vm.shape
    n_heads = o_ref.shape[0] * o_ref.shape[1]
    scale = hd ** -0.5 * LOG2E
    mats = ((wp, rows_p), (wcp, rows_p), (wcq, rows_p), (w1, rows_f), (w2, rows_f))

    def copies(which):
        off = sum(r for _, r in mats[:which])
        dst, rows = mats[which]
        return [pltpu.make_async_copy(g_ref.at[t, pl.ds(off, rows)], dst.at[pl.ds(t * rows, rows)], sems.at[which, t])
                for t in range(tp)]

    if x_ref.shape[0] == n_tok:
        x_src = x_ref
    else:
        x_src = x_ref.at[pl.ds(pl.multiple_of(lax.axis_index("tp") * n_tok, n_tok), n_tok)]
    x_copy = pltpu.make_async_copy(x_src, x_vm, xsem)
    x_copy.start()
    for which in (0, 2, 1, 3, 4):
        for c in copies(which):
            c.start()

    def ready(which):
        for c in copies(which):
            c.wait()

    def mod(i):
        return mod_ref[i:i + 1, :]

    def stack_t(parts):
        return jnp.concatenate(parts, axis=0).T.astype(BF)

    o = stack_t([o_ref[t, h].astype(F32) for t in range(o_ref.shape[0]) for h in range(o_ref.shape[1])])
    ready(0)
    proj = dot(o, wp[...]).astype(BF).astype(F32)
    x_copy.wait()
    x1 = x_vm[...].astype(F32) + mod(2) * proj
    ready(2)
    qt = (dot_nt(x1.astype(BF), wcq[...]) * scale).T
    pad_row = lax.broadcasted_iota(jnp.int32, (80 - hd, n_tok), 0)
    ones_row = jnp.where(pad_row == 0, 1.0, 0.0).astype(BF)
    for h in range(n_heads):
        q_vm[h, :hd, :] = qt[h * hd:(h + 1) * hd, :].astype(BF)
        q_vm[h, hd:, :] = ones_row
    outs = []
    for h in range(n_heads):
        s = dot(kc_ref[h], q_vm[h])
        p = jnp.exp2(s - jnp.max(s, axis=0, keepdims=True)).astype(BF)
        pv = dot(vc_ref[h], p)
        outs.append(pv[:hd] / pv[hd:hd + 1])
    oc = stack_t([v.astype(BF).astype(F32) for v in outs])
    ready(1)
    x2 = x1 + dot(oc, wcp[...]).astype(BF).astype(F32)
    a2 = (layer_norm(x2) * (1.0 + mod(4)) + mod(3)).astype(BF)
    ready(3)
    n_ff = w1.shape[0]
    step = n_ff // 3
    for j in range(3):
        h_vm[:, j * step:(j + 1) * step] = jax.nn.gelu(dot_nt(a2, w1[j * step:(j + 1) * step, :]), approximate=True).astype(BF)
    ready(4)
    x3 = x2 + mod(5) * dot(h_vm[...], w2[...]).astype(BF).astype(F32)
    a = (layer_norm(x3) * (1.0 + mod(7)) + mod(6)).astype(BF)
    if last:
        e_ref[...] = dot(a, wo_ref[...]) + bo_ref[...]
    else:
        xo_ref[...] = x3
        a_ref[...] = a


def token_block(o, x, gathered, kc, vc, mods, w_out, b_out, last):
    tp, n_src_heads, hd, n_tok = o.shape
    dim = x.shape[1]
    rows_p = n_src_heads * hd
    rows_f = (gathered.shape[1] - 3 * rows_p) // 2
    cfg = (tp, hd, rows_p, rows_f, last)
    vmem = pl.BlockSpec(memory_space=pltpu.VMEM)
    hbm = pl.BlockSpec(memory_space=pl.ANY)
    if last:
        out_shape = jax.ShapeDtypeStruct((n_tok, w_out.shape[1]), F32)
        out_specs = vmem
    else:
        out_shape = (jax.ShapeDtypeStruct((n_tok, dim), F32), jax.ShapeDtypeStruct((n_tok, dim), BF))
        out_specs = (vmem, vmem)
    return pl.pallas_call(
        functools.partial(tok_kernel, cfg),
        out_shape=out_shape,
        in_specs=[vmem, hbm, hbm, vmem, vmem, vmem, vmem, vmem],
        out_specs=out_specs,
        scratch_shapes=[
            pltpu.VMEM((tp * rows_p, dim), BF),
            pltpu.VMEM((tp * rows_p, dim), BF),
            pltpu.VMEM((tp * rows_p, dim), BF),
            pltpu.VMEM((tp * rows_f, dim), BF),
            pltpu.VMEM((tp * rows_f, dim), BF),
            pltpu.VMEM((n_tok, dim), x.dtype),
            pltpu.VMEM((n_tok, tp * rows_f), BF),
            pltpu.VMEM((tp * n_src_heads, 80, n_tok), BF),
            pltpu.SemaphoreType.DMA((5, tp)),
            pltpu.SemaphoreType.DMA,
        ],
        compiler_params=pltpu.CompilerParams(vmem_limit_bytes=63 << 20),
        cost_estimate=pl.CostEstimate(flops=20 * 10 ** 9, bytes_accessed=40 * 10 ** 6, transcendentals=0),
    )(o, x, gathered, kc, vc, mods, w_out, b_out)


def solution(mesh):
    row_spec = P(('dp', 'cfg'))
    part_spec = P('dp')
    in_specs = (row_spec, row_spec, row_spec, part_spec, part_spec, part_spec, part_spec, P(),
                P(None, None, None, 'tp'), P(None, 'tp'), P(None, None, 'tp'), P(None, None, None, 'tp'),
                P(None, 'tp'), P(None, None, 'tp'), P(None, 'tp'), P(), P(), P())
    tp = mesh.shape['tp']
    n_cfg = mesh.shape['cfg']

    def local_step(hidden, caption, cap_len, t_block, t_embed, x_t, alpha_bar, mod_table, w_qkv, w_proj, w_cq, w_ckv, w_cproj, w_fc1, w_fc2, final_table, w_out, b_out):
        n_tok, dim = hidden.shape[1:]
        n_layers, _, _, heads, hd = w_qkv.shape
        hw = heads * hd
        row_start = lax.axis_index('cfg') % t_block.shape[0]
        t_rows = lax.dynamic_slice_in_dim(t_block, row_start, 1, axis=0).astype(F32).reshape(6, dim)
        emb = lax.dynamic_slice_in_dim(t_embed, row_start, 1, axis=0).astype(F32)
        fin = final_table.astype(F32) + emb
        mods = [mod_table[l].astype(F32) + t_rows for l in range(n_layers)]
        n_cap = caption.shape[1]
        cap_pad = -(-n_cap // 8) * 8
        key_id = jnp.arange(cap_pad)
        bias = jnp.where(key_id < jnp.minimum(cap_len[0], n_cap), 0.0, -1e30).astype(BF)

        packs, kcs, vcs = [], [], []
        for l in range(n_layers):
            packs.append(jnp.concatenate([
                w_proj[l].reshape(hw, dim), w_cproj[l].reshape(hw, dim), w_cq[l].reshape(dim, hw).T,
                w_fc1[l].T, w_fc2[l]], axis=0))
        gath = [lax.all_gather(p, 'tp', axis=0) for p in packs]
        cap = jnp.pad(caption[0], ((0, cap_pad - n_cap), (0, 0)))
        for l in range(n_layers):
            kv = dot(cap, w_ckv[l].reshape(dim, 2 * hw)).astype(BF)
            kv = lax.all_gather(kv, 'tp', axis=0).reshape(tp, cap_pad, 2, heads, hd)
            k = kv[:, :, 0].transpose(0, 2, 1, 3).reshape(tp * heads, cap_pad, hd)
            k = jnp.concatenate([k, jnp.broadcast_to(bias[None, :, None], (tp * heads, cap_pad, 1)),
                                 jnp.zeros((tp * heads, cap_pad, 80 - hd - 1), BF)], axis=2)
            v = kv[:, :, 1].transpose(0, 2, 3, 1).reshape(tp * heads, hd, cap_pad)
            v = jnp.concatenate([v, jnp.ones((tp * heads, 1, cap_pad), BF), jnp.zeros((tp * heads, 80 - hd - 1, cap_pad), BF)], axis=1)
            kcs.append(k)
            vcs.append(v)

        n_ch = w_out.shape[1] // 4
        keep = n_ch // 2
        w16 = w_out.reshape(dim, 4, n_ch)[:, :, :keep].reshape(dim, 4 * keep)
        w16 = jnp.pad(w16, ((0, 0), (0, 128 - 4 * keep)))
        b16 = jnp.pad(b_out.astype(F32).reshape(4, n_ch)[:, :keep].reshape(1, 4 * keep), ((0, 0), (0, 128 - 4 * keep)))

        src = hidden[0]
        x = src
        for l in range(n_layers):
            o = self_attention(src, mods[l], w_qkv[l].reshape(dim, 3 * hw), tp, heads, hd, l == 0)
            o = lax.all_to_all(o, 'tp', 0, 0, tiled=True)
            last = l == n_layers - 1
            nxt = fin if last else mods[l + 1][:2]
            m8 = jnp.concatenate([mods[l], nxt], axis=0)
            res = token_block(o, x, gath[l], kcs[l], vcs[l], m8, w16, b16, last)
            if not last:
                x, a = res
                src = lax.all_gather(a, 'tp', axis=0, tiled=True)
        eps = lax.all_gather(res[:, :4 * keep], ('cfg', 'tp'), axis=0, tiled=True)
        side = x_t.shape[1]
        g = side // 2
        eps = eps.reshape(n_cfg, g, g, 2, 2, keep).transpose(0, 1, 3, 2, 4, 5).reshape(n_cfg, side, side, keep)
        eu = eps[n_cfg // 2:]
        e = eu + GUIDANCE * (eps[:n_cfg // 2] - eu)
        at = alpha_bar[:, 0][:, None, None, None]
        ap = alpha_bar[:, 1][:, None, None, None]
        x0 = (x_t - jnp.sqrt(1.0 - at) * e) / jnp.sqrt(at)
        return jnp.sqrt(ap) * x0 + jnp.sqrt(1.0 - ap) * e

    return jax.shard_map(local_step, mesh=mesh, in_specs=in_specs, out_specs=part_spec, check_vma=False)
```

time: 1180 us -> 624 us (0.53)
  waiting for transfers between devices: 672 us -> 294 us
  matrix products: 346 us -> 2.45 us
  Pallas kernels: 0 us -> 189 us
  other arithmetic: 116 us -> 8.59 us
  local copies, waits for them, and re-layouts: 21.5 us -> 92 us
    psum x6 -> x0, waiting for transfers between devices: 648 us -> none  [the longest x2 217 us: tp_block(): lax.psum(mlp_part, 'tp').astype(jnp.float32)]
    all_gather x1 -> x6, waiting for transfers between devices: 23.6 us -> 281 us  [the longest x2 183 us: local_step(): gath = [lax.all_gather(p, 'tp', axis=0) for p in packs]]
    pallas_call x0 -> x4, Pallas kernels: none -> 189 us  [the longest x2 110 us: self_attention(): pl.pallas_call(functools.partial(attn_kernel, cfg), out_shape=jax.ShapeDt...]
    dot_general x9 -> x2, matrix products: 174 us -> 2.45 us  [dot(): return jnp.dot(a, b, preferred_element_type=F32)]
    sub x4 -> x0, matrix products: 131 us -> none  [attention(): attn_prob = jax.nn.softmax(scores, axis=-1).astype(jnp.bfloat16)]
    reduce_sum x10 -> x0, other arithmetic: 108 us -> none  [the longest x5 69 us: layer_norm(): mean_val = jnp.mean(values, axis=-1, keepdims=True)]
    slice x5 -> x15, local copies, waits for them, and re-layouts: 2.95 us -> 66.5 us  [the longest x3 31.8 us: local_step(): e = eu + GUIDANCE * (eps[:n_cfg // 2] - eu)]
    unnamed x6 -> x0, matrix products: 41.8 us -> none
  transfers between devices with their start and end apart: 7 -> 8, of which waited for: 7 -> 5; matrix products, arithmetic and copies ran while one was open for 0% -> 5% of each run, Pallas kernels for 0% -> 18%
where the time goes in v1:
time: 624 us; the launch traced here: 612 us
  waiting for transfers between devices  294 us (47%)
  Pallas kernels  189 us (30%)
  local copies, waits for them, and re-layouts  92 us (15%)
  between operations  14.7 us (2%)
  starting transfers between devices  11.3 us (2%)
  other arithmetic  8.59 us (1%)
    all_gather x2, waiting for transfers between devices, local_step(): gath = [lax.all_gather(p, 'tp', axis=0) for p in packs]  183 us
    pallas_call x2, Pallas kernels, self_attention(): pl.pallas_call(functools.partial(attn_kernel, cfg), out_shape=jax.ShapeDt...  110 us
    pallas_call x2, Pallas kernels, token_block(): pl.pallas_call(functools.partial(tok_kernel, cfg), out_shape=out_shape, i...  78.8 us
    all_gather x1, waiting for transfers between devices, local_step(): src = lax.all_gather(a, 'tp', axis=0, tiled=True)  49.1 us
    all_gather x1, waiting for transfers between devices, local_step(): eps = lax.all_gather(res[:, :4 * keep], ('cfg', 'tp'), axis=0, tiled=True)  48.2 us
    slice x3, local copies, waits for them, and re-layouts, local_step(): e = eu + GUIDANCE * (eps[:n_cfg // 2] - eu)  31.8 us
    slice x2, local copies, waits for them, and re-layouts, local_step(): eu = eps[n_cfg // 2:]  27.5 us
  transfers between devices with their start and end apart: 8, of which 5 were waited for; matrix products, arithmetic and copies ran while one was open for 5% of the time, Pallas kernels for 18%

profile of v1, /device:TPU:98, one launch (start us, length us, event | category | flops | bytes accessed | tf_op | source)
XLA Modules:
  0.0 612.0 jit_solution(3792052653720043969)
XLA Ops:
  6.6 1.5 fusion.15
  8.1 1.2 fusion.2
  9.4 1.2 fusion.3
  15.0 1.7 bitcast_dynamic-update-slice_fusion
  16.6 1.0 copy-done.2
  17.7 1.7 bitcast_dynamic-update-slice_fusion.2
  21.0 1.1 fusion.12
  22.1 1.6 copy.63.w_ref
  24.4 57.1 %shard_map.172 = bf16[8,2,72,512]{3,2,1,0:T(8,128)(2,1)} custom-call(bf16[4096,1152]{1,0:T(8,128)(2,1)} %bitcast.107, f32[6,1152]{1,0:T(8,128)} %get-tuple-element.36.mod_ref, bf16[1152,432]{1,0:T(8,128)(2,1)} %copy.63.w_ref), custom_call_target="tpu_custom_call" | custom-call | flops 30000001024 | bytes 20000000 | tf_op jit(solution)/shard_map/pallas_call | solution.py:106
  81.5 5.3 all-to-all-start
  90.0 1.6 fusion.14
  92.4 2.8 fusion.13
  95.3 2.2 copy.83
  97.5 3.0 maximum_maximum_fusion.1
  100.7 2.6 fusion.1
  103.4 12.2 %all-to-all-done.o_ref = bf16[8,2,72,512]{3,2,1,0:T(8,128)(2,1)} async-done(((bf16[8,2,72,512]{3,2,1,0:T(8,128)(2,1)}), bf16[8,2,72,512]{3,2,1,0:T(8,128)(2,1)}, u32[]{:S(2)}, u32[]{:S(2)}) %all-to-all-start) | async-done | bytes 1179680 | tf_op jit(solution)/shard_map/all_to_all | solution.py:286
  115.6 92.8 %all-gather.17.cloned.1.call-done = bf16[12672,1152]{1,0:T(8,128)(2,1)} async-done(((bf16[1584,1152]{1,0:T(8,128)(2,1)}), bf16[12672,1152]{1,0:T(8,128)(2,1)}) %all-gather.17.cloned.1.call-update) | async-done | bytes 29196304 | tf_op jit(solution)/shard_map/all_gather | solution.py:263
  208.4 39.6 %shard_map.173 = (f32[512,1152]{1,0:T(8,128)}, bf16[512,1152]{1,0:T(8,128)(2,1)}) custom-call(bf16[8,2,72,512]{3,2,1,0:T(8,128)(2,1)} %all-to-all-done.o_ref, bf16[4096,1152]{1,0:T(8,128)(2,1)} %bitcast.108, bf16[8,1584,1152]{2,1,0:T(8,128)(2,1)} %bitcast.105, bf16[16,304,80]{2,1,0:T(8,128)(2,1)} %get-tuple-element.28.kc_ref, ...), custom_call_target="tpu_custom_call" | custom-call | flops 20000000000 | bytes 40000000 | tf_op jit(solution)/shard_map/pallas_call | solution.py:213
  249.2 1.6 copy.68.w_ref
  250.8 49.1 %all-gather.13.cloned.1.call-done.src_ref = bf16[4096,1152]{1,0:T(8,128)(2,1)} async-done(((bf16[512,1152]{1,0:T(8,128)(2,1)}), bf16[4096,1152]{1,0:T(8,128)(2,1)}) %all-gather.13.cloned.1.call-update) | async-done | bytes 9437200 | tf_op jit(solution)/shard_map/all_gather | solution.py:293
  299.9 53.4 %shard_map.174 = bf16[8,2,72,512]{3,2,1,0:T(8,128)(2,1)} custom-call(bf16[4096,1152]{1,0:T(8,128)(2,1)} %all-gather.13.cloned.1.call-done.src_ref, f32[6,1152]{1,0:T(8,128)} %copy-done.8, bf16[1152,432]{1,0:T(8,128)(2,1)} %copy.68.w_ref), custom_call_target="tpu_custom_call" | custom-call | flops 30000001024 | bytes 20000000 | tf_op jit(solution)/shard_map/pallas_call | solution.py:106
  353.3 5.4 all-to-all-start.1
  359.8 90.6 %all-gather.19.cloned.1.call-done = bf16[12672,1152]{1,0:T(8,128)(2,1)} async-done(((bf16[1584,1152]{1,0:T(8,128)(2,1)}), bf16[12672,1152]{1,0:T(8,128)(2,1)}) %all-gather.19.cloned.1.call-update) | async-done | bytes 29196304 | tf_op jit(solution)/shard_map/all_gather | solution.py:263
  450.4 39.2 %shard_map.175 = f32[512,128]{1,0:T(8,128)} custom-call(bf16[8,2,72,512]{3,2,1,0:T(8,128)(2,1)} %all-to-all-done.1.o_ref, f32[512,1152]{1,0:T(8,128)} %get-tuple-element.8.x_ref, bf16[8,1584,1152]{2,1,0:T(8,128)(2,1)} %bitcast.106, bf16[16,304,80]{2,1,0:T(8,128)(2,1)} %get-tuple-element.27.kc_ref, bf16[16,80,304]{2,1,0:T(8,128)(2,1)} %get-tuple-element.39.vc_ref, ...), custom_call_target="tpu_custom_call" | custom-call | flops 20000000000 | bytes 40000000 | tf_op jit(solution)/shard_map/pallas_call | solution.py:213
  489.9 48.2 %all-gather.15.cloned.1.call-done = f32[16384,16]{1,0:T(8,128)} async-done(((f32[512,16]{1,0:T(8,128)}), f32[16384,16]{1,0:T(8,128)}) %all-gather.15.cloned.1.call-update) | async-done | bytes 1048592 | tf_op jit(solution)/shard_map/all_gather | solution.py:294
  538.1 5.3 copy.71
  544.3 1.2 fusion.11
  545.4 20.6 %copy.73 = f32[2,64,2,64,2,4]{5,4,3,2,1,0:T(2,128)} copy(f32[2,64,2,64,2,4]{3,1,0,5,4,2:T(8,128)} %get-tuple-element.17) | data formatting | bytes 1048576 | tf_op jit(solution)/shard_map/slice | solution.py:299
  566.1 10.0 %copy.74 = f32[2,128,128,4]{2,1,3,0:T(8,128)S(1)} copy(f32[2,128,128,4]{3,2,1,0:T(8,128)} %bitcast.84) | data formatting | bytes 1048576 | tf_op jit(solution)/shard_map/slice | solution.py:299
  576.1 17.4 %copy.72 = f32[2,64,2,64,2,4]{5,4,3,2,1,0:T(2,128)} copy(f32[2,64,2,64,2,4]{3,1,0,5,4,2:T(8,128)S(1)} %get-tuple-element.18) | data formatting | bytes 1048576 | tf_op jit(solution)/shard_map/slice | solution.py:298
  593.5 10.1 %copy.76 = f32[2,128,128,4]{2,1,3,0:T(8,128)S(1)} copy(f32[2,128,128,4]{3,2,1,0:T(8,128)} %bitcast.85) | data formatting | bytes 1048576 | tf_op jit(solution)/shard_map/slice | solution.py:298
  603.8 1.1 copy.78
  (85 shorter events, 13.8 us)
Async XLA Ops:
  6.5 1.5 copy-start.17
  6.5 83.4 %all-gather.21.cloned.1.call-start = ((), (), s32[]{:S(2)}) async-start(), calls=%async_computation.6 | async-start | bytes 1990656 | tf_op jit(solution)/shard_map/all_gather | solution.py:267
  8.0 2.8 copy-start.4
  8.1 3.6 copy-start.5
  9.4 83.1 %all-gather.23.cloned.1.call-start = ((), (), s32[]{:S(2)}) async-start(), calls=%async_computation.7 | async-start | bytes 1990656 | tf_op jit(solution)/shard_map/all_gather | solution.py:267
  10.7 3.3 copy-start.6
  10.7 197.7 %all-gather.17.cloned.1.call-start = ((), (), s32[]{:S(2)}) async-start(), calls=%async_computation.4 | async-start | bytes 32845824 | tf_op jit(solution)/shard_map/all_gather | solution.py:263
  11.7 3.2 copy-start.1
  15.0 2.7 copy-start.2
  19.4 0.7 copy-start.12
  19.4 1.6 copy-start.3
  21.0 2.8 copy-start.11
  24.4 62.4 %copy-start.8 = (f32[6,1152]{1,0:T(8,128)}, f32[6,1152]{1,0:T(8,128)S(1)}, u32[]{:S(2)}) copy-start(f32[6,1152]{1,0:T(8,128)S(1)} %get-tuple-element.35.mod_ref) | copy-start | bytes 82948
  24.4 63.2 %copy-start.13 = (bf16[1152,32]{0,1:T(8,128)(2,1)S(1)}, bf16[1152,32]{0,1:T(8,128)(2,1)}, u32[]{:S(2)}) copy-start(bf16[1152,32]{0,1:T(8,128)(2,1)} %param.34) | copy-start | bytes 221188
  81.5 7.2 %copy-start.18 = (bf16[32]{0:T(256)(128)(2,1)S(1)}, bf16[32]{0:T(256)(128)(2,1)}, u32[]{:S(2)}) copy-start(bf16[32]{0:T(256)(128)(2,1)} %param.35) | copy-start | bytes 196
  81.5 7.9 %copy-start.10 = (f32[6,1152]{1,0:T(8,128)S(1)}, f32[6,1152]{1,0:T(8,128)}, u32[]{:S(2)}) copy-start(f32[6,1152]{1,0:T(8,128)} %get-tuple-element.36.mod_ref) | copy-start | bytes 82948
  81.5 34.1 %all-to-all-start = ((bf16[8,2,72,512]{3,2,1,0:T(8,128)(2,1)}), bf16[8,2,72,512]{3,2,1,0:T(8,128)(2,1)}, u32[]{:S(2)}, u32[]{:S(2)}) async-start(bf16[8,2,72,512]{3,2,1,0:T(8,128)(2,1)} %shard_map.172), calls=%async_computation | async-start | bytes 2359296 | tf_op jit(solution)/shard_map/all_to_all | solution.py:286
  86.8 213.1 %all-gather.13.cloned.1.call-start = ((), (), s32[]{:S(2)}) async-start(), calls=%async_computation.2 | async-start | bytes 10616832 | tf_op jit(solution)/shard_map/all_gather | solution.py:293
  248.0 1.2 copy-start
  248.0 202.4 %all-gather.19.cloned.1.call-start = ((), (), s32[]{:S(2)}) async-start(), calls=%async_computation.5 | async-start | bytes 32845824 | tf_op jit(solution)/shard_map/all_gather | solution.py:263
  250.8 108.3 %copy-start.14 = (bf16[2,1152]{1,0:T(2,128)(2,1)S(1)}, bf16[2,1152]{1,0:T(2,128)(2,1)}, u32[]{:S(2)}) copy-start(bf16[2,1152]{1,0:T(2,128)(2,1)} %param.22) | copy-start | bytes 13828
  250.8 108.4 %copy-start.15 = (bf16[2,1152]{1,0:T(2,128)(2,1)S(1)}, bf16[2,1152]{1,0:T(2,128)(2,1)}, u32[]{:S(2)}) copy-start(bf16[2,1152]{1,0:T(2,128)(2,1)} %param.33) | copy-start | bytes 13828
  250.8 108.4 %copy-start.9 = (f32[6,1152]{1,0:T(8,128)S(1)}, f32[6,1152]{1,0:T(8,128)}, u32[]{:S(2)}) copy-start(f32[6,1152]{1,0:T(8,128)} %copy-done.8) | copy-start | bytes 82948
  353.3 97.1 %all-to-all-start.1 = ((bf16[8,2,72,512]{3,2,1,0:T(8,128)(2,1)}), bf16[8,2,72,512]{3,2,1,0:T(8,128)(2,1)}, u32[]{:S(2)}, u32[]{:S(2)}) async-start(bf16[8,2,72,512]{3,2,1,0:T(8,128)(2,1)} %shard_map.174), calls=%async_computation.1 | async-start | bytes 2359296 | tf_op jit(solution)/shard_map/all_to_all | solution.py:286
  358.7 179.4 %all-gather.15.cloned.1.call-start = ((), (), s32[]{:S(2)}) async-start(), calls=%async_computation.3 | async-start | bytes 8650752 | tf_op jit(solution)/shard_map/all_gather | solution.py:294
  450.4 39.3 %copy-start.16 = (f32[2,2]{1,0:T(2,128)S(1)}, f32[2,2]{1,0:T(2,128)}, u32[]{:S(2)}) copy-start(f32[2,2]{1,0:T(2,128)} %param.24) | copy-start | bytes 52
  593.5 10.1 %copy-start.7 = (f32[2,128,128,4]{2,3,1,0:T(4,128)S(1)}, f32[2,128,128,4]{2,3,1,0:T(4,128)}, u32[]{:S(2)}) copy-start(f32[2,128,128,4]{2,3,1,0:T(4,128)} %param.23) | copy-start | bytes 1572868
Sparse Core Ops, SparseCore 0:
  9.5 23.4 all-gather.20
  34.5 22.2 all-gather.22
  58.4 149.9 all-gather.16
  248.1 51.6 all-gather.12
  301.3 149.0 all-gather.18
  489.8 48.2 all-gather.14
